TPU v7x, 32 devices: a whole 2x2x4 slice. The times are simulated.
32 devices in a mesh: outer: 2 (over core), dp: 4 (over z), tensor: 4 (over y, x).
Axes of the slice: x: 2, y: 2, z: 4, core: 2. Of those that a mesh axis runs over, the one named last changes fastest.
Arguments:
- attn: bfloat16 [2048, 8192], P(('outer', 'dp'), 'tensor'), may hold values from -6 to 6
- out_weight: bfloat16 [8192, 8192], P(None, 'tensor'), may hold values from -0.0625 to 0.0625
- resid: bfloat16 [2048, 8192], P(('outer', 'dp'), 'tensor'), may hold values from -8 to 8
- norm_gain: bfloat16 [8192], P('tensor'), may hold values from 0.5 to 1.5
- head: bfloat16 [8192], P('tensor'), may hold values from -1 to 1
- lengths: int32 [32], P(('outer', 'dp')), may hold values from 1 to 64
- pairs: int32 [32, 2], P(('outer', 'dp')), may hold values from 0 to 3, as said below
- pair_valid: int32 [32], P(('outer', 'dp')), may hold values from 0 to 1, as said below
- loss_scale: float32 [1], replicated, may hold values from 1024 to 8192
Outputs:
- loss: float32 [1], replicated
- grad_out_proj: float32 [8192, 8192], P(('outer', 'dp'), 'tensor')
- grad_gain: float32 [8192], P('tensor')
- grad_head: float32 [8192], P('tensor')
Inputs may be any that keep to these rules, and one draw needn't show every extreme that they name: `pairs`: in each pair the two numbers differ; the first pair of each replica is valid. `pair_valid`: the first of each replica's 4 entries is 1.
All inputs are finite; a program needn't handle non-finite values.
Results may differ from a plain program's by a relative error of at most 0.003.
Values may be sent and summed in bfloat16 or wider, within the bound.
A program may use at most 128 MiB of HBM per device.

v0:
```python
import jax
import jax.numpy as jnp
from jax import lax
from jax.sharding import PartitionSpec as P


def shards(attn, out_weight, resid, norm_gain, head, lengths, pairs, pair_valid, loss_scale):
    f32 = jnp.float32
    tok_dev = attn.shape[0]
    feats = resid.shape[1]
    tensor = lax.axis_size("tensor")
    width = feats * tensor
    seqs_dev = lengths.shape[0]
    seq_len = tok_dev // seqs_dev
    valid = pair_valid.astype(f32)
    count = lax.psum(jnp.sum(valid), ("outer", "dp"))
    part = lax.dot_general(out_weight, attn, (((1,), (1,)), ((), ())), preferred_element_type=f32)
    part = part.astype(jnp.bfloat16).reshape(tensor, feats, tok_dev)
    part = lax.all_to_all(part, "tensor", split_axis=0, concat_axis=0, tiled=True)
    z = resid.astype(f32).T + jnp.sum(part.astype(f32), axis=0)
    gain = norm_gain.astype(f32)[:, None]
    headv = head.astype(f32)[:, None]
    both = headv * gain
    sums = lax.psum(jnp.stack([jnp.sum(z * z, axis=0), jnp.sum(z * both, axis=0)]), "tensor")
    inv = 1.0 / jnp.sqrt(sums[0] / width + 1e-05)
    score = sums[1] * inv
    position = jnp.arange(tok_dev)
    seq_of = position // seq_len
    within = position % seq_len
    member = (within[:, None] < lengths[None, :]) & (
        seq_of[:, None] == jnp.arange(seqs_dev)[None, :]
    )
    pooling = member.astype(f32) / lengths.astype(f32)[None, :]
    reward = jnp.sum(pooling * score[:, None], axis=0)
    choose = jnp.arange(seqs_dev)[None, :]
    select = (pairs[:, 0:1] == choose).astype(f32) - (pairs[:, 1:2] == choose).astype(f32)
    margin = jnp.sum(select * reward[None, :], axis=1)
    loss_part = jnp.sum(valid * jax.nn.softplus(-margin))
    dmargin = -loss_scale[0] * valid * jax.nn.sigmoid(-margin) / count
    dreward = jnp.sum(dmargin[:, None] * select, axis=0)
    dscore = jnp.sum(pooling * dreward[None, :], axis=1)
    weight = inv * dscore
    dproj = weight[None, :] * both - z * (inv**3 * dscore * sums[1] / width)[None, :]
    dproj = dproj.astype(jnp.bfloat16)
    zsum = jnp.sum(z * weight[None, :], axis=1)
    gathered = lax.all_gather(dproj, "tensor", axis=0, tiled=True)
    exchanged = lax.all_to_all(gathered, ("outer", "dp"), split_axis=0, concat_axis=1, tiled=True)
    grad_out_proj = jnp.dot(
        exchanged,
        lax.all_gather(attn, ("outer", "dp"), axis=0, tiled=True),
        preferred_element_type=f32,
    )
    zsum, loss_sum = lax.psum((zsum, loss_part), ("outer", "dp"))
    loss = (loss_sum / count).reshape(1)
    return (loss, grad_out_proj, zsum * headv[:, 0], zsum * gain[:, 0])


def solution(mesh):
    return jax.shard_map(
        shards,
        mesh=mesh,
        in_specs=(
            P(("outer", "dp"), "tensor"),
            P(None, "tensor"),
            P(("outer", "dp"), "tensor"),
            P("tensor"),
            P("tensor"),
            P(("outer", "dp")),
            P(("outer", "dp"), None),
            P(("outer", "dp")),
            P(),
        ),
        out_specs=(P(), P(("outer", "dp"), "tensor"), P("tensor"), P("tensor")),
        check_vma=False,
    )
```

profile of v0, /device:TPU:0, one launch (start us, length us, event | category | flops | bytes accessed | tf_op | source)
XLA Modules:
  0.0 368.8 jit_solution(16129040595212171715)
XLA Ops:
  7.2 16.7 %convolution_convert_fusion = bf16[8192,256]{1,0:T(8,128)(2,1)} fusion(bf16[8192,2048]{1,0:T(8,128)(2,1)} %param.10, bf16[256,2048]{1,0:T(8,128)(2,1)} %param.9), kind=kOutput, calls=%fused_computation | convolution fusion | flops 8592031744 | bytes 38797312 | tf_op jit(solution)/shard_map/dot_general | solution.py:17
  23.9 0.0 copy-start
  23.9 0.0 copy-start.3
  23.9 0.0 copy-start.5
  23.9 0.0 copy-start.1
  23.9 0.0 copy-start.2
  23.9 5.3 %all-to-all-start = ((bf16[4,2048,256]{2,1,0:T(8,128)(2,1)}), bf16[4,2048,256]{2,1,0:T(8,128)(2,1)}, u32[]{:S(2)}, u32[]{:S(2)}) async-start(bf16[4,2048,256]{2,1,0:T(8,128)(2,1)} %bitcast.31), calls=%async_computation | async-start | bytes 8388608 | tf_op jit(solution)/shard_map/all_to_all | solution.py:19
  29.3 0.0 all-gather.3.cloned.1.call-start
  29.3 0.0 copy-done
  29.3 0.5 copy.15
  29.8 0.0 copy-done.3
  30.5 0.0 copy-done.5
  30.5 0.0 copy-done.1
  30.5 0.0 copy-done.2
  30.6 0.0 copy-start.4
  30.6 47.4 %all-to-all-done = bf16[4,2048,256]{2,1,0:T(8,128)(2,1)} async-done(((bf16[4,2048,256]{2,1,0:T(8,128)(2,1)}), bf16[4,2048,256]{2,1,0:T(8,128)(2,1)}, u32[]{:S(2)}, u32[]{:S(2)}) %all-to-all-start) | async-done | bytes 4194336 | tf_op jit(solution)/shard_map/all_to_all | solution.py:19
  77.9 3.0 convert_reduce_fusion
  80.9 0.5 multiply_reduce_fusion.2
  81.4 8.9 %psum.28 = f32[2,256]{1,0:T(2,128)S(1)} all-reduce(f32[2,256]{1,0:T(2,128)S(1)} %pad_maximum_fusion), channel_id=1, replica_groups=mesh['outer'=2,'dp'=4,'tensor'=4] {'tensor'}, use_global_device_ids=true, to_apply=%region_3.0 | all-reduce | flops 512 | bytes 4096 | tf_op jit(solution)/shard_map/psum | solution.py:24
  90.3 0.2 multiply_reduce_fusion.4
  90.5 0.2 multiply_reduce_fusion.6
  90.7 0.0 copy-done.4
  90.7 0.6 convert_reduce_fusion.1
  91.3 16.2 %psum.30 = f32[]{:T(128)} all-reduce(f32[]{:T(128)} %get-tuple-element.6), channel_id=1, replica_groups=mesh['outer'=2,'dp'=4,'tensor'=4] {'outer','dp'}, use_global_device_ids=true, to_apply=%region_9.10 | all-reduce | flops 1 | bytes 8 | tf_op jit(solution)/shard_map/psum | solution.py:16
  107.5 0.7 fusion.9
  108.2 0.1 multiply_reduce_fusion.5
  108.3 0.1 multiply_reduce_fusion.3
  108.4 1.5 subtract_convert_fusion
  109.9 0.0 all-gather.3.cloned.1.call-update
  109.9 0.0 all-gather.5.cloned.1.call-start
  110.0 0.7 all-gather.5.cloned.1.call-update
  110.7 50.8 %all-gather.3.cloned.1.call-done = bf16[8192,256]{1,0:T(8,128)(2,1)} async-done(((bf16[2048,256]{1,0:T(8,128)(2,1)}), bf16[8192,256]{1,0:T(8,128)(2,1)}) %all-gather.3.cloned.1.call-update) | async-done | bytes 4194320 | tf_op jit(solution)/shard_map/all_gather | solution.py:46
  161.5 4.6 %all-to-all-start.1 = ((bf16[8,1024,256]{2,1,0:T(8,128)(2,1)}), bf16[8,1024,256]{2,1,0:T(8,128)(2,1)}, u32[]{:S(2)}, u32[]{:S(2)}) async-start(bf16[8,1024,256]{2,1,0:T(8,128)(2,1)} %bitcast.30), calls=%async_computation.1 | async-start | bytes 8388608 | tf_op jit(solution)/shard_map/all_to_all | solution.py:47
  166.1 171.7 %all-reduce = (f32[]{:T(128)}, f32[2048]{0:T(1024)S(1)}) all-reduce(f32[]{:T(128)} %get-tuple-element.7, f32[2048]{0:T(1024)S(1)} %get-tuple-element.11), channel_id=1, replica_groups=mesh['outer'=2,'dp'=4,'tensor'=4] {'outer','dp'}, use_global_device_ids=true, to_apply=%region_7.8 | all-reduce | flops 2049 | bytes 16392 | tf_op jit(solution)/shard_map/psum | solution.py:53
  339.1 0.6 convert_multiply_fusion
  339.7 0.0 all-to-all-done.1
  339.7 6.5 %copy.16 = bf16[1024,8,256]{0,2,1:T(8,128)(2,1)} copy(bf16[1024,8,256]{2,0,1:T(8,128)(2,1)} %bitcast.13) | data formatting | bytes 8388608 | tf_op jit(solution)/shard_map/all_to_all | solution.py:47
  346.2 0.0 all-gather.5.cloned.1.call-done
  346.2 14.6 %fusion.11 = f32[1024,2048]{1,0:T(8,128)} fusion(bf16[1024,2048]{0,1:T(8,128)(2,1)} %bitcast.32, bf16[2048,2048]{1,0:T(8,128)(2,1)} %all-gather.5.cloned.1.call-done), kind=kOutput, calls=%fused_computation.44 | convolution fusion | flops 8589934592 | bytes 20971520 | tf_op jit(solution)/shard_map/dot_general | solution.py:48
  (7 shorter events, 0.1 us)
Async XLA Ops:
  23.9 5.4 %copy-start = (bf16[256,2048]{1,0:T(8,128)(2,1)S(1)}, bf16[256,2048]{1,0:T(8,128)(2,1)}, u32[]{:S(2)}) copy-start(bf16[256,2048]{1,0:T(8,128)(2,1)} %param.11) | copy-start | bytes 3145732
  23.9 5.9 %copy-start.3 = (s32[4]{0:T(128)S(1)}, s32[4]{0:T(128)}, u32[]{:S(2)}) copy-start(s32[4]{0:T(128)} %param.14) | copy-start | bytes 52
  23.9 6.6 %copy-start.5 = (s32[4,2]{0,1:T(2,128)S(1)}, s32[4,2]{0,1:T(2,128)}, u32[]{:S(2)}) copy-start(s32[4,2]{0,1:T(2,128)} %param.15) | copy-start | bytes 100
  23.9 6.6 %copy-start.1 = (bf16[2048]{0:T(1024)(128)(2,1)S(1)}, bf16[2048]{0:T(1024)(128)(2,1)}, u32[]{:S(2)}) copy-start(bf16[2048]{0:T(1024)(128)(2,1)} %param.12) | copy-start | bytes 12292
  23.9 6.6 %copy-start.2 = (bf16[2048]{0:T(1024)(128)(2,1)S(1)}, bf16[2048]{0:T(1024)(128)(2,1)}, u32[]{:S(2)}) copy-start(bf16[2048]{0:T(1024)(128)(2,1)} %param.13) | copy-start | bytes 12292
  23.9 54.0 %all-to-all-start = ((bf16[4,2048,256]{2,1,0:T(8,128)(2,1)}), bf16[4,2048,256]{2,1,0:T(8,128)(2,1)}, u32[]{:S(2)}, u32[]{:S(2)}) async-start(bf16[4,2048,256]{2,1,0:T(8,128)(2,1)} %bitcast.31), calls=%async_computation | async-start | bytes 8388608 | tf_op jit(solution)/shard_map/all_to_all | solution.py:19
  29.3 132.2 %all-gather.3.cloned.1.call-start = ((), (), s32[]{:S(2)}) async-start(), calls=%async_computation.2 | async-start | bytes 5242880 | tf_op jit(solution)/shard_map/all_gather | solution.py:46
  30.6 60.2 %copy-start.4 = (s32[4]{0:T(128)S(1)}, s32[4]{0:T(128)}, u32[]{:S(2)}) copy-start(s32[4]{0:T(128)} %param.16) | copy-start | bytes 52
  109.9 236.3 %all-gather.5.cloned.1.call-start = ((), (), s32[]{:S(2)}) async-start(), calls=%async_computation.3 | async-start | bytes 9437184 | tf_op jit(solution)/shard_map/all_gather | solution.py:50
  161.5 178.2 %all-to-all-start.1 = ((bf16[8,1024,256]{2,1,0:T(8,128)(2,1)}), bf16[8,1024,256]{2,1,0:T(8,128)(2,1)}, u32[]{:S(2)}, u32[]{:S(2)}) async-start(bf16[8,1024,256]{2,1,0:T(8,128)(2,1)} %bitcast.30), calls=%async_computation.1 | async-start | bytes 8388608 | tf_op jit(solution)/shard_map/all_to_all | solution.py:47
Sparse Core Ops, SparseCore 0:
  110.0 51.4 all-gather.2
  163.1 160.7 all-gather.4
where the time goes:
time: 369 us
  blocking collectives  197 us (53%)
  waiting for transfers between devices  98.9 us (27%)
  matrix products  31.4 us (9%)
  between operations  17.3 us (5%)
  starting transfers between devices  9.99 us (3%)
  other arithmetic  7.44 us (2%)
  local copies, waits for them, and re-layouts  7.01 us (2%)
    psum x1, blocking collectives, shards(): zsum, loss_sum = lax.psum((zsum, loss_part), ('outer', 'dp'))  172 us
    all_gather x1, waiting for transfers between devices, shards(): gathered = lax.all_gather(dproj, 'tensor', axis=0, tiled=True)  50.8 us
    all_to_all x1, waiting for transfers between devices, shards(): lax.all_to_all(part, 'tensor', split_axis=0, concat_axis=0, tiled=True)  47.4 us
    dot_general x1, matrix products, shards(): lax.dot_general(out_weight, attn, (((1,), (1,)), ((), ())), preferred_ele...  16.7 us
    psum x1, blocking collectives, shards(): count = lax.psum(jnp.sum(valid), ('outer', 'dp'))  16.2 us
    dot_general x1, matrix products, shards(): jnp.dot(exchanged, lax.all_gather(attn, ('outer', 'dp'), axis=0, tiled=Tr...  14.6 us
    psum x1, blocking collectives, shards(): lax.psum(jnp.stack([jnp.sum(z * z, axis=0), jnp.sum(z * both, axis=0)]),...  8.91 us
  transfers between devices with their start and end apart: 4, of which 2 were waited for; matrix products, arithmetic and copies ran while one was open for 2% of the time, Pallas kernels for 0%

commit v1 on v0

--- a/solution.py
+++ b/solution.py
@@ -2,6 +2,28 @@
 import jax.numpy as jnp
 from jax import lax
 from jax.sharding import PartitionSpec as P
+
+
+def laid_out(blocks, dim):
+    blocks = jnp.moveaxis(blocks, 0, dim)
+    shape = blocks.shape
+    return blocks.reshape(*shape[:dim], shape[dim] * shape[dim + 1], *shape[dim + 2 :])
+
+
+def collect(value, axis, dim):
+    size = lax.axis_size(axis)
+    pairs = [(i, (i + 1) % size) for i in range(size)]
+    back = [(b, a) for a, b in pairs]
+    lower, upper = ([], [])
+    for step in range(size - 1):
+        if step % 2 == 0:
+            lower.append(lax.ppermute(lower[-1] if lower else value, axis, pairs))
+        else:
+            upper.append(lax.ppermute(upper[-1] if upper else value, axis, back))
+    blocks = jnp.stack([*lower[::-1], value, *upper])
+    shift = lax.axis_index(axis) - len(lower)
+    blocks = blocks[(jnp.arange(size) - shift) % size]
+    return laid_out(blocks, dim)
 
 
 def shards(attn, out_weight, resid, norm_gain, head, lengths, pairs, pair_valid, loss_scale):
@@ -43,7 +65,7 @@
     dproj = weight[None, :] * both - z * (inv**3 * dscore * sums[1] / width)[None, :]
     dproj = dproj.astype(jnp.bfloat16)
     zsum = jnp.sum(z * weight[None, :], axis=1)
-    gathered = lax.all_gather(dproj, "tensor", axis=0, tiled=True)
+    gathered = collect(dproj, "tensor", 0)
     exchanged = lax.all_to_all(gathered, ("outer", "dp"), split_axis=0, concat_axis=1, tiled=True)
     grad_out_proj = jnp.dot(
         exchanged,

time: 369 us -> 335 us (0.908)
  blocking collectives: 197 us -> 134 us
  waiting for transfers between devices: 98.9 us -> 116 us
  local copies, waits for them, and re-layouts: 7.01 us -> 12 us
    ppermute x0 -> x3, waiting for transfers between devices: none -> 68.9 us  [the longest x2 46.6 us: collect(): lower.append(lax.ppermute(lower[-1] if lower else value, axis, pairs))]
    psum x1, blocking collectives: 172 us -> 104 us  [shards(): zsum, loss_sum = lax.psum((zsum, loss_part), ('outer', 'dp'))]
    all_gather x1 -> x0, waiting for transfers between devices: 50.8 us -> none  [shards(): gathered = lax.all_gather(dproj, 'tensor', axis=0, tiled=True)]
    gather x0 -> x1, local copies, waits for them, and re-layouts: none -> 4.96 us  [collect(): blocks = blocks[(jnp.arange(size) - shift) % size]]
    psum x1, blocking collectives: 16.2 us -> 20.6 us  [shards(): count = lax.psum(jnp.sum(valid), ('outer', 'dp'))]
  transfers between devices with their start and end apart: 4 -> 6, of which waited for: 2 -> 4; matrix products, arithmetic and copies ran while one was open for 2% -> 7% of each run, Pallas kernels for 0% -> 0%
where the time goes in v1:
time: 335 us; the launch traced here: 334 us
  blocking collectives  134 us (40%)
  waiting for transfers between devices  116 us (35%)
  matrix products  31.4 us (9%)
  between operations  17.3 us (5%)
  starting transfers between devices  12.9 us (4%)
  local copies, waits for them, and re-layouts  12 us (4%)
  other arithmetic  10.8 us (3%)
    psum x1, blocking collectives, shards(): zsum, loss_sum = lax.psum((zsum, loss_part), ('outer', 'dp'))  104 us
    ppermute x2, waiting for transfers between devices, collect(): lower.append(lax.ppermute(lower[-1] if lower else value, axis, pairs))  46.6 us
    all_to_all x1, waiting for transfers between devices, shards(): lax.all_to_all(part, 'tensor', split_axis=0, concat_axis=0, tiled=True)  46.6 us
    ppermute x1, waiting for transfers between devices, collect(): upper.append(lax.ppermute(upper[-1] if upper else value, axis, back))  22.4 us
    psum x1, blocking collectives, shards(): count = lax.psum(jnp.sum(valid), ('outer', 'dp'))  20.6 us
    dot_general x1, matrix products, shards(): lax.dot_general(out_weight, attn, (((1,), (1,)), ((), ())), preferred_ele...  16.7 us
    dot_general x1, matrix products, shards(): jnp.dot(exchanged, lax.all_gather(attn, ('outer', 'dp'), axis=0, tiled=Tr...  14.6 us
    psum x1, blocking collectives, shards(): lax.psum(jnp.stack([jnp.sum(z * z, axis=0), jnp.sum(z * both, axis=0)]),...  8.97 us
  transfers between devices with their start and end apart: 6, of which 4 were waited for; matrix products, arithmetic and copies ran while one was open for 7% of the time, Pallas kernels for 0%

profile of v1, /device:TPU:0, one launch (start us, length us, event | category | flops | bytes accessed | tf_op | source)
XLA Modules:
  0.0 334.3 jit_solution(6699907102236108869)
XLA Ops:
  7.2 16.7 %convolution_convert_fusion = bf16[8192,256]{1,0:T(8,128)(2,1)} fusion(bf16[8192,2048]{1,0:T(8,128)(2,1)} %param.10, bf16[256,2048]{1,0:T(8,128)(2,1)} %param.9), kind=kOutput, calls=%fused_computation.1 | convolution fusion | flops 8592031744 | bytes 38797312 | tf_op jit(solution)/shard_map/dot_general | solution.py:39
  23.9 0.0 copy-start
  23.9 0.0 copy-start.3
  23.9 0.0 copy-start.5
  23.9 0.0 copy-start.1
  23.9 0.0 copy-start.2
  23.9 5.3 %all-to-all-start = ((bf16[4,2048,256]{2,1,0:T(8,128)(2,1)}), bf16[4,2048,256]{2,1,0:T(8,128)(2,1)}, u32[]{:S(2)}, u32[]{:S(2)}) async-start(bf16[4,2048,256]{2,1,0:T(8,128)(2,1)} %bitcast.37), calls=%async_computation | async-start | bytes 8388608 | tf_op jit(solution)/shard_map/all_to_all | solution.py:41
  29.3 0.0 all-gather.2.cloned.1.call-start
  29.3 0.7 all-gather.2.cloned.1.call-update
  30.0 0.0 copy-done
  30.0 0.5 copy.16
  30.6 0.0 copy-done.3
  31.2 0.0 copy-done.5
  31.3 0.0 copy-done.1
  31.3 0.0 copy-done.2
  31.3 0.0 copy-start.4
  31.3 46.6 %all-to-all-done = bf16[4,2048,256]{2,1,0:T(8,128)(2,1)} async-done(((bf16[4,2048,256]{2,1,0:T(8,128)(2,1)}), bf16[4,2048,256]{2,1,0:T(8,128)(2,1)}, u32[]{:S(2)}, u32[]{:S(2)}) %all-to-all-start) | async-done | bytes 4194336 | tf_op jit(solution)/shard_map/all_to_all | solution.py:41
  77.9 3.0 convert_reduce_fusion
  80.9 0.4 multiply_reduce_fusion.2
  81.3 9.0 %psum.28 = f32[2,256]{1,0:T(2,128)S(1)} all-reduce(f32[2,256]{1,0:T(2,128)S(1)} %pad_maximum_fusion.1), channel_id=1, replica_groups=mesh['outer'=2,'dp'=4,'tensor'=4] {'tensor'}, use_global_device_ids=true, to_apply=%region_3.0 | all-reduce | flops 512 | bytes 4096 | tf_op jit(solution)/shard_map/psum | solution.py:46
  90.3 0.2 multiply_reduce_fusion.4
  90.5 0.2 multiply_reduce_fusion.6
  90.7 0.0 copy-done.4
  90.7 0.6 convert_reduce_fusion.1
  91.3 20.6 %psum.30 = f32[]{:T(128)} all-reduce(f32[]{:T(128)} %get-tuple-element.6), channel_id=1, replica_groups=mesh['outer'=2,'dp'=4,'tensor'=4] {'outer','dp'}, use_global_device_ids=true, to_apply=%region_9.10 | all-reduce | flops 1 | bytes 8 | tf_op jit(solution)/shard_map/psum | solution.py:38
  111.9 0.7 fusion.11
  112.5 0.1 multiply_reduce_fusion.5
  112.6 0.1 multiply_reduce_fusion.3
  112.7 1.5 subtract_convert_fusion
  114.3 0.0 collective-permute-start
  114.3 2.9 collective-permute-start.2
  117.2 24.0 %collective-permute-done = bf16[2048,256]{1,0:T(8,128)(2,1)S(1)} collective-permute-done((bf16[2048,256]{1,0:T(8,128)(2,1)}, bf16[2048,256]{1,0:T(8,128)(2,1)S(1)}, u32[]{:S(2)}, u32[]{:S(2)}) %collective-permute-start) | collective-permute-done | bytes 1048608 | tf_op jit(solution)/shard_map/ppermute | solution.py:20
  141.2 0.0 collective-permute-start.1
  141.3 22.4 %collective-permute-done.2 = bf16[2048,256]{1,0:T(8,128)(2,1)S(1)} collective-permute-done((bf16[2048,256]{1,0:T(8,128)(2,1)}, bf16[2048,256]{1,0:T(8,128)(2,1)S(1)}, u32[]{:S(2)}, u32[]{:S(2)}) %collective-permute-start.2) | collective-permute-done | bytes 1048608 | tf_op jit(solution)/shard_map/ppermute | solution.py:22
  163.6 22.6 %collective-permute-done.1 = bf16[2048,256]{1,0:T(8,128)(2,1)S(1)} collective-permute-done((bf16[2048,256]{1,0:T(8,128)(2,1)S(1)}, bf16[2048,256]{1,0:T(8,128)(2,1)S(1)}, u32[]{:S(2)}, u32[]{:S(2)}) %collective-permute-start.1) | collective-permute-done | bytes 1048608 | tf_op jit(solution)/shard_map/ppermute | solution.py:20
  186.2 3.3 pad_maximum_fusion
  189.5 5.0 %gather_fusion = bf16[4,2048,256]{2,1,0:T(8,128)(2,1)} fusion(bf16[4,2048,256]{2,1,0:T(8,128)(2,1)} %pad_maximum_fusion, s32[1024]{0:T(1024)S(1)} %pad_clamp_fusion), kind=kCustom, calls=%fused_computation | custom fusion | bytes 8388624 | tf_op jit(solution)/shard_map/gather | solution.py:25
  194.5 4.6 %all-to-all-start.1 = ((bf16[8,1024,256]{2,1,0:T(8,128)(2,1)}), bf16[8,1024,256]{2,1,0:T(8,128)(2,1)}, u32[]{:S(2)}, u32[]{:S(2)}) async-start(bf16[8,1024,256]{2,1,0:T(8,128)(2,1)} %bitcast.36), calls=%async_computation.1 | async-start | bytes 8388608 | tf_op jit(solution)/shard_map/all_to_all | solution.py:69
  199.1 104.2 %all-reduce = (f32[]{:T(128)}, f32[2048]{0:T(1024)S(1)}) all-reduce(f32[]{:T(128)} %get-tuple-element.7, f32[2048]{0:T(1024)S(1)} %get-tuple-element.11), channel_id=1, replica_groups=mesh['outer'=2,'dp'=4,'tensor'=4] {'outer','dp'}, use_global_device_ids=true, to_apply=%region_7.8 | all-reduce | flops 2049 | bytes 16392 | tf_op jit(solution)/shard_map/psum | solution.py:75
  304.6 0.6 convert_multiply_fusion
  305.2 0.0 all-to-all-done.1
  305.2 6.5 %copy.17 = bf16[1024,8,256]{0,2,1:T(8,128)(2,1)} copy(bf16[1024,8,256]{2,0,1:T(8,128)(2,1)} %bitcast.18) | data formatting | bytes 8388608 | tf_op jit(solution)/shard_map/all_to_all | solution.py:69
  311.7 0.0 all-gather.2.cloned.1.call-done
  311.7 14.6 %fusion.13 = f32[1024,2048]{1,0:T(8,128)} fusion(bf16[1024,2048]{0,1:T(8,128)(2,1)} %bitcast.38, bf16[2048,2048]{1,0:T(8,128)(2,1)} %all-gather.2.cloned.1.call-done), kind=kOutput, calls=%fused_computation.53 | convolution fusion | flops 8589934592 | bytes 20971520 | tf_op jit(solution)/shard_map/dot_general | solution.py:70
  (9 shorter events, 0.1 us)
Async XLA Ops:
  23.9 6.1 %copy-start = (bf16[256,2048]{1,0:T(8,128)(2,1)S(1)}, bf16[256,2048]{1,0:T(8,128)(2,1)}, u32[]{:S(2)}) copy-start(bf16[256,2048]{1,0:T(8,128)(2,1)} %param.11) | copy-start | bytes 3145732
  23.9 6.6 %copy-start.3 = (s32[4]{0:T(128)S(1)}, s32[4]{0:T(128)}, u32[]{:S(2)}) copy-start(s32[4]{0:T(128)} %param.14) | copy-start | bytes 52
  23.9 7.3 %copy-start.5 = (s32[4,2]{0,1:T(2,128)S(1)}, s32[4,2]{0,1:T(2,128)}, u32[]{:S(2)}) copy-start(s32[4,2]{0,1:T(2,128)} %param.15) | copy-start | bytes 100
  23.9 7.3 %copy-start.1 = (bf16[2048]{0:T(1024)(128)(2,1)S(1)}, bf16[2048]{0:T(1024)(128)(2,1)}, u32[]{:S(2)}) copy-start(bf16[2048]{0:T(1024)(128)(2,1)} %param.12) | copy-start | bytes 12292
  23.9 7.3 %copy-start.2 = (bf16[2048]{0:T(1024)(128)(2,1)S(1)}, bf16[2048]{0:T(1024)(128)(2,1)}, u32[]{:S(2)}) copy-start(bf16[2048]{0:T(1024)(128)(2,1)} %param.13) | copy-start | bytes 12292
  23.9 53.9 %all-to-all-start = ((bf16[4,2048,256]{2,1,0:T(8,128)(2,1)}), bf16[4,2048,256]{2,1,0:T(8,128)(2,1)}, u32[]{:S(2)}, u32[]{:S(2)}) async-start(bf16[4,2048,256]{2,1,0:T(8,128)(2,1)} %bitcast.37), calls=%async_computation | async-start | bytes 8388608 | tf_op jit(solution)/shard_map/all_to_all | solution.py:41
  29.3 282.4 %all-gather.2.cloned.1.call-start = ((), (), s32[]{:S(2)}) async-start(), calls=%async_computation.2 | async-start | bytes 9437184 | tf_op jit(solution)/shard_map/all_gather | solution.py:72
  31.3 59.4 %copy-start.4 = (s32[4]{0:T(128)S(1)}, s32[4]{0:T(128)}, u32[]{:S(2)}) copy-start(s32[4]{0:T(128)} %param.16) | copy-start | bytes 52
  114.3 27.0 %collective-permute-start = (bf16[2048,256]{1,0:T(8,128)(2,1)}, bf16[2048,256]{1,0:T(8,128)(2,1)S(1)}, u32[]{:S(2)}, u32[]{:S(2)}) collective-permute-start(bf16[2048,256]{1,0:T(8,128)(2,1)} %get-tuple-element.10), channel_id=1, source_target_pairs={{0,1},{1,2},{2,3},{3,0},{4,5},{5,6},{6,7},{7,4},{8,9},{9,10},{10,1... | collective-permute-start | bytes 3145736 | tf_op jit(solution)/shard_map/ppermute | solution.py:20
  114.3 49.3 %collective-permute-start.2 = (bf16[2048,256]{1,0:T(8,128)(2,1)}, bf16[2048,256]{1,0:T(8,128)(2,1)S(1)}, u32[]{:S(2)}, u32[]{:S(2)}) collective-permute-start(bf16[2048,256]{1,0:T(8,128)(2,1)} %get-tuple-element.10), channel_id=1, source_target_pairs={{1,0},{2,1},{3,2},{0,3},{5,4},{6,5},{7,6},{4,7},{9,8},{10,9},{11,1... | collective-permute-start | bytes 3145736 | tf_op jit(solution)/shard_map/ppermute | solution.py:22
  141.2 44.9 %collective-permute-start.1 = (bf16[2048,256]{1,0:T(8,128)(2,1)S(1)}, bf16[2048,256]{1,0:T(8,128)(2,1)S(1)}, u32[]{:S(2)}, u32[]{:S(2)}) collective-permute-start(bf16[2048,256]{1,0:T(8,128)(2,1)S(1)} %collective-permute-done), channel_id=1, source_target_pairs={{0,1},{1,2},{2,3},{3,0},{4,5},{5,6},{6,7},{7,4},{8,9},{9,10},{10,1... | collective-permute-start | bytes 3145736 | tf_op jit(solution)/shard_map/ppermute | solution.py:20
  194.5 110.7 %all-to-all-start.1 = ((bf16[8,1024,256]{2,1,0:T(8,128)(2,1)}), bf16[8,1024,256]{2,1,0:T(8,128)(2,1)}, u32[]{:S(2)}, u32[]{:S(2)}) async-start(bf16[8,1024,256]{2,1,0:T(8,128)(2,1)} %bitcast.36), calls=%async_computation.1 | async-start | bytes 8388608 | tf_op jit(solution)/shard_map/all_to_all | solution.py:69
Sparse Core Ops, SparseCore 0:
  31.7 85.4 all-gather.1
